TPU v7x, 256 devices: a whole 4x4x8 slice. The times are simulated.
256 devices in a mesh: nodes: 64 (over z, x, core), heads: 4 (over y).
Axes of the slice: x: 4, y: 4, z: 8, core: 2. Of those that a mesh axis runs over, the one named last changes fastest.
Arguments:
- nodes_in: bfloat16 [32768, 1024], P('nodes', 'heads'), may hold values from -6 to 6
- local_gain: float32 [1024], replicated, may hold values from 0.5 to 1.5
- neighbour_query_key_value: bfloat16 [3, 1024, 1024], P(None, None, 'heads'), may hold values from -0.25 to 0.25
- local_out: bfloat16 [1024, 1024], P('heads'), may hold values from -0.1875 to 0.1875
- global_gain: float32 [1024], replicated, may hold values from 0.5 to 1.5
- global_qkv: bfloat16 [3, 1024, 1024], P(None, None, 'heads'), may hold values from -0.1875 to 0.1875
- global_out: bfloat16 [1024, 1024], P('heads'), may hold values from -1.875 to 1.875
- feature_map: bfloat16 [16, 64, 128], P('heads'), may hold values from -5 to 5
- neighbour_count: int32 [256], P('nodes'), may hold values from 1 to 8
- neighbour_blocks: int32 [256, 8], P('nodes'), may hold values from 0 to 255, as said below
- metis_order: int32 [256], P('nodes'), may hold values from 0 to 255, as said below
- hashed_order: int32 [256], P('nodes'), may hold values from 0 to 255, as said below
Outputs:
- output: bfloat16 [32768, 1024], P('nodes', 'heads')
Inputs may be any that keep to these rules, and one draw needn't show every extreme that they name: `neighbour_blocks`: entry 0 of block b's list is b itself; every entry lies within 2 blocks of the aligned group of 4 blocks that holds b, inside the graph; entries from neighbour_count on are unused; entries may repeat. `metis_order`: A permutation of the block ids. `hashed_order`: A permutation of the block ids. The blocks at the 4 METIS positions of aligned group g go to the aligned groups of 4 hashed positions numbered (g + k * 16) modulo 64 for k = 0 to 3, exactly 1 of them to each; which block goes to which of these groups, and to which position in it, is drawn.
All inputs are finite; a program needn't handle non-finite values.
Results may differ from a plain program's by a relative error of at most 0.015.
Values may be sent and summed in bfloat16 or wider, within the bound.
No kernel may reach another device: no remote copies, remote signals or barrier semaphores. Data moves between devices by JAX's collectives and lax.ppermute only.
A program may use at most 64 MiB of HBM per device.

v0:
```python
import jax
import jax.numpy as jnp
from jax import lax
from jax.sharding import PartitionSpec as P

HD = 64
BLOCK = 128
HALO_BLK = 2
EPSILON = 1e-06


def passed_along(value, axis, steps):
    count = lax.axis_size(axis)
    pairs = [(source, (source + steps) % count) for source in range(count)]
    return lax.ppermute(value, axis, pairs)


def gathered_total(array, axis):
    parts = lax.all_gather(array, axis)
    return parts.sum(axis=0)


def laid_out(parts, dim):
    parts = jnp.moveaxis(parts, 0, dim)
    dims = parts.shape
    return parts.reshape(*dims[:dim], dims[dim] * dims[dim + 1], *dims[dim + 2 :])


def copy_for_each(array, axis):
    copies = jnp.broadcast_to(array, (lax.axis_size(axis), *array.shape))
    return lax.all_to_all(copies, axis, split_axis=0, concat_axis=0, tiled=True)


def collect(array, axis, dim):
    return laid_out(copy_for_each(array, axis), dim)


def padded(array, sides, width):
    for axis, dim in sides:
        count, length = (lax.axis_size(axis), array.shape[dim])
        up = [(i, (i + 1) % count) for i in range(count - 1)]
        down = [(j, i) for i, j in up]
        last = lax.slice_in_dim(array, length - width, length, axis=dim)
        initial = lax.slice_in_dim(array, 0, width, axis=dim)
        before = lax.ppermute(last, axis, up)
        after = lax.ppermute(initial, axis, down)
        array = jnp.concatenate([before, array, after], axis=dim)
    return array


def cut_along(array, dim, count):
    dims = array.shape
    parts = array.reshape(*dims[:dim], count, dims[dim] // count, *dims[dim + 1 :])
    return jnp.moveaxis(parts, dim, 0)


def summed_on_arrival(array, axis, dim):
    count = lax.axis_size(axis)
    parts = lax.all_to_all(cut_along(array, dim, count), axis, 0, 0, tiled=True)
    return jnp.sum(parts.astype(jnp.float32), axis=0)


def root_scale(row_data, gain_vector):
    as_float = row_data.astype(jnp.float32)
    mean_square = jnp.mean(as_float * as_float, axis=-1, keepdims=True)
    return (as_float * lax.rsqrt(mean_square + EPSILON) * gain_vector).astype(jnp.bfloat16)


def local_attention(queries, extended, counts, local_index):
    block_count = counts.shape[0]
    list_slots = local_index.shape[1]
    group_size = 4
    feature_width = queries.shape[1]
    heads_local = feature_width // HD
    key_blocks = extended.reshape(2, -1, BLOCK, feature_width)
    query_groups = queries.reshape(block_count // group_size, group_size, BLOCK, heads_local, HD)
    slot_of_key = jnp.arange(list_slots * BLOCK, dtype=jnp.int32) // BLOCK

    def one_group(inputs):
        query_group, index_group, count_group = inputs
        picked = key_blocks[:, index_group].reshape(
            2, group_size, list_slots * BLOCK, heads_local, HD
        )
        scores = jnp.einsum(
            "gqhd,gkhd->ghqk", query_group, picked[0], preferred_element_type=jnp.float32
        ) * HD ** (-0.5)
        live = slot_of_key[None, :] < count_group[:, None]
        scores = jnp.where(live[:, None, None, :], scores, -jnp.inf)
        row_max = jnp.max(scores, axis=-1, keepdims=True)
        expo = jnp.exp(scores - row_max)
        totals = jnp.sum(expo, axis=-1)
        local_weights = expo.astype(jnp.bfloat16)
        mixed_heads = jnp.einsum(
            "ghqk,gkhd->gqhd", local_weights, picked[1], preferred_element_type=jnp.float32
        )
        mixed_heads = mixed_heads / jnp.transpose(totals, (0, 2, 1))[..., None]
        return mixed_heads.astype(jnp.bfloat16)

    mixed_all = lax.map(
        one_group,
        (
            query_groups,
            local_index.reshape(block_count // group_size, group_size, list_slots),
            counts.reshape(block_count // group_size, group_size),
        ),
    )
    return mixed_all.reshape(block_count * BLOCK, feature_width)


def relayout(row_data, metis_local, all_hashed, device_nodes):
    block_count = metis_local.shape[0]
    devices = lax.axis_size("nodes")
    lane_count = min(block_count, devices)
    stride = max(1, devices // block_count)
    slot_limit = block_count // lane_count
    feature_width = row_data.shape[1]
    total_blocks = all_hashed.shape[0]
    matches = all_hashed[None, :] == metis_local[:, None]
    target = jnp.sum(
        jnp.where(matches, jnp.arange(total_blocks, dtype=jnp.int32)[None, :], 0), axis=1
    )
    steps_away = (target // block_count - device_nodes) % devices // stride
    order_ids = jnp.arange(block_count, dtype=jnp.int32)
    earlier = (steps_away[None, :] == steps_away[:, None]) & (
        order_ids[None, :] < order_ids[:, None]
    )
    rank_within = jnp.sum(earlier.astype(jnp.int32), axis=1)
    lane_id = rank_within * lane_count + steps_away
    chosen = lane_id[None, :] == order_ids[:, None]
    source = jnp.sum(jnp.where(chosen, order_ids[None, :], 0), axis=1)
    lane_target = jnp.sum(jnp.where(chosen, target[None, :], 0), axis=1)
    blocks = row_data.reshape(block_count, BLOCK, feature_width)
    outgoing = blocks[source].reshape(slot_limit, lane_count, BLOCK, feature_width)
    positions = lane_target.reshape(slot_limit, lane_count)
    block_pieces = [outgoing[:, :1]]
    position_pieces = [positions[:, :1]]
    for lane_step in range(1, lane_count):
        arrived, arrived_at = passed_along(
            (outgoing[:, lane_step : lane_step + 1], positions[:, lane_step : lane_step + 1]),
            "nodes",
            lane_step * stride,
        )
        block_pieces.append(arrived)
        position_pieces.append(arrived_at)
    incoming = jnp.concatenate(block_pieces, axis=1)
    in_position = jnp.concatenate(position_pieces, axis=1)
    local_position = in_position.reshape(block_count) - device_nodes * block_count
    located = local_position[None, :] == order_ids[:, None]
    picked_lane = jnp.sum(jnp.where(located, order_ids[None, :], 0), axis=1)
    return incoming.reshape(block_count, BLOCK, feature_width)[picked_lane].reshape(
        block_count * BLOCK, feature_width
    )


def gather_rows(shard_rows):
    return lax.all_gather(shard_rows, "heads", axis=1, tiled=True)


def global_mixing(full_rows, gain_vector, triple_weight, feature_map, out_weight):
    rescaled_input = root_scale(full_rows, gain_vector)
    triple = jnp.einsum(
        "au,nuz->naz", rescaled_input, triple_weight, preferred_element_type=jnp.float32
    ).astype(jnp.bfloat16)
    row_count = full_rows.shape[0]
    heads_local = feature_map.shape[0]

    def feature_maps(head_rows):
        angles = jnp.einsum(
            "nhd,hdf->nhf",
            head_rows.reshape(row_count, heads_local, HD),
            feature_map,
            preferred_element_type=jnp.float32,
        ) * HD ** (-0.5)
        return (jax.nn.elu(angles) + 1.0).astype(jnp.bfloat16)

    phi_query = feature_maps(triple[0])
    phi_key = feature_maps(triple[1])
    head_values = triple[2].reshape(row_count, heads_local, HD)
    summary = jnp.einsum("nhf,nhd->hfd", phi_key, head_values, preferred_element_type=jnp.float32)
    key_total = jnp.sum(phi_key.astype(jnp.float32), axis=0)
    summary, key_total = (gathered_total(summary, "nodes"), gathered_total(key_total, "nodes"))
    query_float = phi_query.astype(jnp.float32)
    numerator = jnp.einsum("nhf,hfd->nhd", query_float, summary, precision=lax.Precision.HIGHEST)
    denominator = jnp.einsum("nhf,hf->nh", query_float, key_total, precision=lax.Precision.HIGHEST)
    global_mixed = (
        (numerator / denominator[..., None])
        .astype(jnp.bfloat16)
        .reshape(row_count, heads_local * HD)
    )
    return jnp.dot(global_mixed, out_weight, preferred_element_type=jnp.float32)


def body(
    nodes_in,
    local_gain,
    neighbour_query_key_value,
    local_out,
    global_gain,
    global_qkv,
    global_out,
    feature_map,
    neighbour_count,
    neighbour_blocks,
    metis_order,
    hashed_order,
):
    block_count = metis_order.shape[0]
    device_nodes = lax.axis_index("nodes")
    all_hashed = collect(hashed_order, "nodes", 0)
    full_input = collect(nodes_in, "heads", 1)
    local_rescaled = root_scale(full_input, local_gain)
    triple = jnp.einsum(
        "au,nuz->naz", local_rescaled, neighbour_query_key_value, preferred_element_type=jnp.float32
    ).astype(jnp.bfloat16)
    rim_rows = HALO_BLK * BLOCK
    extended = padded(triple[1:], (("nodes", 1),), rim_rows)
    first_block = device_nodes * block_count - HALO_BLK
    local_index = neighbour_blocks - first_block
    local_mixed = local_attention(triple[0], extended, neighbour_count, local_index)
    partial_value = jnp.dot(local_mixed, local_out, preferred_element_type=jnp.float32)
    summed = lax.psum_scatter(
        partial_value.astype(jnp.bfloat16), "heads", scatter_dimension=1, tiled=True
    ).astype(jnp.float32)
    hidden = (nodes_in.astype(jnp.float32) + summed).astype(jnp.bfloat16)
    full_rows = gather_rows(hidden)
    global_partial = global_mixing(full_rows, global_gain, global_qkv, feature_map, global_out)
    global_summed = summed_on_arrival(global_partial.astype(jnp.bfloat16), "heads", 1)
    result = (hidden.astype(jnp.float32) + global_summed).astype(jnp.bfloat16)
    result = relayout(result, metis_order, all_hashed, device_nodes)
    return result


def solution(mesh):
    in_specs = (
        P("nodes", "heads"),
        P(),
        P(None, None, "heads"),
        P("heads", None),
        P(),
        P(None, None, "heads"),
        P("heads", None),
        P("heads", None, None),
        P("nodes"),
        P("nodes", None),
        P("nodes"),
        P("nodes"),
    )
    out_specs = P("nodes", "heads")
    return jax.shard_map(body, mesh=mesh, in_specs=in_specs, out_specs=out_specs, check_vma=False)
```

profile of v0, /device:TPU:33, one launch (start us, length us, event | category | flops | bytes accessed | tf_op | source)
XLA Modules:
  0.0 270.1 jit_solution(14255202605277190932)
XLA Ops:
  8.7 4.2 %all-to-all-start = ((bf16[4,512,256]{2,1,0:T(8,128)(2,1)}), bf16[4,512,256]{2,1,0:T(8,128)(2,1)}, u32[]{:S(2)}, u32[]{:S(2)}) async-start(bf16[4,512,256]{2,1,0:T(8,128)(2,1)} %broadcast_in_dim.96), calls=%async_computation | async-start | bytes 2097152 | tf_op jit(solution)/shard_map/all_to_all | solution.py:31
  13.1 14.1 %all-to-all-done = bf16[4,512,256]{2,1,0:T(8,128)(2,1)} async-done(((bf16[4,512,256]{2,1,0:T(8,128)(2,1)}), bf16[4,512,256]{2,1,0:T(8,128)(2,1)}, u32[]{:S(2)}, u32[]{:S(2)}) %all-to-all-start) | async-done | bytes 1048608 | tf_op jit(solution)/shard_map/all_to_all | solution.py:31
  30.5 3.7 %collective-permute-start.1 = (bf16[2,256,256]{2,1,0:T(8,128)(2,1)S(1)}, bf16[2,256,256]{2,1,0:T(8,128)(2,1)S(1)}, u32[]{:S(2)}, u32[]{:S(2)}) collective-permute-start(bf16[2,256,256]{2,1,0:T(8,128)(2,1)S(1)} %get-tuple-element.34), channel_id=1, source_target_pairs={{4,0},{8,4},{12,8},{16,12},{20,16},{24,20},{28,24},{32,28},{36,32}... | collective-permute-start | bytes 786440 | tf_op jit(solution)/shard_map/ppermute | solution.py:46
  34.2 3.0 %collective-permute-start = (bf16[2,256,256]{2,1,0:T(8,128)(2,1)S(1)}, bf16[2,256,256]{2,1,0:T(8,128)(2,1)}, u32[]{:S(2)}, u32[]{:S(2)}) collective-permute-start(bf16[2,256,256]{2,1,0:T(8,128)(2,1)S(1)} %get-tuple-element.33), channel_id=1, source_target_pairs={{0,4},{4,8},{8,12},{12,16},{16,20},{20,24},{24,28},{28,32},{32,36}... | collective-permute-start | bytes 786440 | tf_op jit(solution)/shard_map/ppermute | solution.py:45
  41.7 2.8 %gather_fusion = bf16[32,2,128,256]{3,2,1,0:T(8,128)(2,1)} fusion(bf16[2,8,128,256]{3,2,1,0:T(8,128)(2,1)S(1)} %bitcast.121, s32[1024]{0:T(1024)S(1)} %pad_clamp_fusion.2), kind=kCustom, calls=%fused_computation | custom fusion | bytes 8388736 | tf_op jit(solution)/shard_map/while/body/eval_jaxpr/gather | solution.py:81
  44.5 7.5 %copy.37 = bf16[4,8,2,128,256]{3,1,4,0,2:T(8,128)(2,1)} copy(bf16[4,8,2,128,256]{4,3,2,1,0:T(8,128)(2,1)} %bitcast.122) | data formatting | bytes 8388608 | tf_op jit(solution)/shard_map/while/body/eval_jaxpr/gather | solution.py:81
  52.0 4.5 %fusion.50 = (bf16[1,4,8,128,256]{3,2,4,1,0:T(8,128)(2,1)}, bf16[1,4,8,128,256]{3,2,4,1,0:T(8,128)(2,1)}) fusion(bf16[2,4,8,128,256]{3,2,4,1,0:T(8,128)(2,1)} %bitcast.123), kind=kLoop, calls=%fused_computation.104 | loop fusion | bytes 8388608 | tf_op jit(solution)/shard_map/while/body/eval_jaxpr/slice | solution.py:85
  56.5 4.2 %squeeze.19 = bf16[4,1024,4,64]{1,3,2,0:T(8,128)(2,1)} reshape(bf16[1,4,8,128,256]{3,2,4,1,0:T(8,128)(2,1)} %get-tuple-element.20) | data formatting | bytes 4194304 | tf_op jit(solution)/shard_map/while/body/eval_jaxpr/squeeze | solution.py:94
  60.7 4.2 %squeeze.21 = bf16[4,1024,4,64]{1,3,2,0:T(8,128)(2,1)} reshape(bf16[1,4,8,128,256]{3,2,4,1,0:T(8,128)(2,1)} %get-tuple-element.19) | data formatting | bytes 4194304 | tf_op jit(solution)/shard_map/while/body/eval_jaxpr/squeeze | solution.py:85
  64.8 2.9 %fusion = (f32[4,4,128]{2,1,0:T(4,128)S(1)}, f32[4,4,128,1024]{3,2,1,0:T(8,128)S(1)}) fusion(pred[4,1024]{1,0:T(4,128)(4,1)S(1)} %broadcast_compare_fusion, bf16[4,1024,4,64]{1,3,2,0:T(8,128)(2,1)} %squeeze.21, bf16[4,128,4,64]{3,2,1,0:T(4,128)(2,1)S(1)} %reshape.297), kind=kOutput, calls=%fused_computation.5 | convolution fusion | flops 274724864 | bytes 10760192 | tf_op jit(solution)/shard_map/while/body/eval_jaxpr/gqhd,gkhd->ghqk/dot_general | solution.py:84
  73.9 27.8 %reduce-scatter.2.cloned.1.call-done = bf16[512,256]{1,0:T(8,128)(2,1)} async-done(((bf16[512,1024]{1,0:T(8,128)(2,1)}), bf16[512,256]{1,0:T(8,128)(2,1)}) %reduce-scatter.2.cloned.1.call-update) | async-done | bytes 262160 | tf_op jit(solution)/shard_map/reduce_scatter | solution.py:221
  103.4 28.0 %all-gather.6.cloned.1.call-done = bf16[512,1024]{1,0:T(8,128)(2,1)} async-done(((bf16[512,256]{1,0:T(8,128)(2,1)}), bf16[512,1024]{1,0:T(8,128)(2,1)}) %all-gather.6.cloned.1.call-update) | async-done | bytes 1048592 | tf_op jit(solution)/shard_map/all_gather | solution.py:156
  132.9 2.4 fusion.14
  137.2 20.2 %all_to_all.16 = s32[64,1,4]{2,1,0:T(1,128)S(1)} all-to-all(s32[64,1,4]{2,1,0:T(1,128)S(1)} %broadcast_in_dim.100), channel_id=1, replica_groups=mesh['nodes'=64,'heads'=4] {'nodes'}, dimensions={0} | all-to-all | bytes 2048 | tf_op jit(solution)/shard_map/all_to_all | solution.py:31
  159.4 48.5 %all-gather.2 = f32[64,4,128]{2,1,0:T(4,128)S(1)} all-gather(f32[1,4,128]{2,1,0:T(4,128)S(1)} %bitcast.138), channel_id=3, replica_groups=mesh['nodes'=64,'heads'=4] {'nodes'}, dimensions={0}, use_global_device_ids=true | all-gather | bytes 133120 | tf_op jit(solution)/shard_map/all_gather | solution.py:19
  209.3 13.4 %all-gather.8.cloned.1.call-done = f32[256,128,64]{1,2,0:T(8,128)} async-done(((f32[4,128,64]{1,2,0:T(8,128)}), f32[256,128,64]{1,2,0:T(8,128)}) %all-gather.8.cloned.1.call-update) | async-done | bytes 8388624 | tf_op jit(solution)/shard_map/all_gather | solution.py:19
  222.7 3.9 %reduce_sum.116 = f32[4,128,64]{1,2,0:T(8,128)S(1)} reduce(f32[64,4,128,64]{2,3,1,0:T(8,128)} %bitcast.124, f32[]{:T(128)} %constant.91.clone.1), dimensions={0}, to_apply=%region_5.6 | reduce | flops 2064384 | bytes 8519684 | tf_op jit(solution)/shard_map/reduce_sum | solution.py:20
  229.1 4.2 %all-to-all-start.1 = ((bf16[4,512,256]{2,1,0:T(8,128)(2,1)}), bf16[4,512,256]{2,1,0:T(8,128)(2,1)S(1)}, u32[]{:S(2)}, u32[]{:S(2)}) async-start(bf16[4,512,256]{2,1,0:T(8,128)(2,1)} %bitcast.126), calls=%async_computation.2 | async-start | bytes 2097152 | tf_op jit(solution)/shard_map/all_to_all | solution.py:59
  235.8 3.3 %collective-permute-start.6 = (s32[1,1]{1,0:T(1,128)}, s32[1,1]{1,0:T(1,128)}, u32[]{:S(2)}, u32[]{:S(2)}) collective-permute-start(s32[1,1]{1,0:T(1,128)} %get-tuple-element.41), channel_id=1, source_target_pairs={{0,128},{4,132},{8,136},{12,140},{16,144},{20,148},{24,152},{28,15... | collective-permute-start | bytes 20 | tf_op jit(solution)/shard_map/ppermute | solution.py:15
  239.1 3.2 %collective-permute-done.6 = s32[1,1]{1,0:T(1,128)} collective-permute-done((s32[1,1]{1,0:T(1,128)}, s32[1,1]{1,0:T(1,128)}, u32[]{:S(2)}, u32[]{:S(2)}) %collective-permute-start.6) | collective-permute-done | bytes 36 | tf_op jit(solution)/shard_map/ppermute | solution.py:15
  243.9 2.6 add_subtract_fusion
  250.7 3.3 %collective-permute-start.3 = (bf16[1,1,128,256]{3,2,1,0:T(8,128)(2,1)S(1)}, bf16[1,1,128,256]{3,2,1,0:T(8,128)(2,1)S(1)}, u32[]{:S(2)}, u32[]{:S(2)}) collective-permute-start(bf16[1,1,128,256]{3,2,1,0:T(8,128)(2,1)S(1)} %get-tuple-element.37), channel_id=1, source_target_pairs={{0,128},{4,132},{8,136},{12,140},{16,144},{20,148},{24,152},{28,15... | collective-permute-start | bytes 196616 | tf_op jit(solution)/shard_map/ppermute | solution.py:15
  254.0 4.9 %collective-permute-done.3 = bf16[1,1,128,256]{3,2,1,0:T(8,128)(2,1)S(1)} collective-permute-done((bf16[1,1,128,256]{3,2,1,0:T(8,128)(2,1)S(1)}, bf16[1,1,128,256]{3,2,1,0:T(8,128)(2,1)S(1)}, u32[]{:S(2)}, u32[]{:S(2)}) %collective-permute-start.3) | collective-permute-done | bytes 65568 | tf_op jit(solution)/shard_map/ppermute | solution.py:15
  258.9 3.4 %collective-permute-done.2 = bf16[1,1,128,256]{3,2,1,0:T(8,128)(2,1)S(1)} collective-permute-done((bf16[1,1,128,256]{3,2,1,0:T(8,128)(2,1)S(1)}, bf16[1,1,128,256]{3,2,1,0:T(8,128)(2,1)S(1)}, u32[]{:S(2)}, u32[]{:S(2)}) %collective-permute-start.2) | collective-permute-done | bytes 65568 | tf_op jit(solution)/shard_map/ppermute | solution.py:15
  (98 shorter events, 36.4 us)
Async XLA Ops:
  6.5 22.8 %copy-start = (bf16[3,1024,256]{2,1,0:T(8,128)(2,1)S(1)}, bf16[3,1024,256]{2,1,0:T(8,128)(2,1)}, u32[]{:S(2)}) copy-start(bf16[3,1024,256]{2,1,0:T(8,128)(2,1)} %param.14) | copy-start | bytes 4718596
  6.5 6.5 %copy-start.7 = (s32[4,8]{1,0:T(4,128)S(1)}, s32[4,8]{1,0:T(4,128)}, u32[]{:S(2)}) copy-start(s32[4,8]{1,0:T(4,128)} %param.21) | copy-start | bytes 388
  8.7 18.6 %all-to-all-start = ((bf16[4,512,256]{2,1,0:T(8,128)(2,1)}), bf16[4,512,256]{2,1,0:T(8,128)(2,1)}, u32[]{:S(2)}, u32[]{:S(2)}) async-start(bf16[4,512,256]{2,1,0:T(8,128)(2,1)} %broadcast_in_dim.96), calls=%async_computation | async-start | bytes 2097152 | tf_op jit(solution)/shard_map/all_to_all | solution.py:31
  13.0 16.1 %copy-start.6 = (f32[1024]{0:T(1024)S(1)}, f32[1024]{0:T(1024)}, u32[]{:S(2)}) copy-start(f32[1024]{0:T(1024)} %param.13) | copy-start | bytes 12292
  13.0 88.7 %reduce-scatter.2.cloned.1.call-start = ((), (), s32[]{:S(2)}) async-start(), calls=%async_computation.4 | async-start | bytes 1310720 | tf_op jit(solution)/shard_map/reduce_scatter | solution.py:221
  29.4 7.9 %copy-start.9 = (s32[4]{0:T(128)S(1)}, s32[4]{0:T(128)}, u32[]{:S(2)}) copy-start(s32[4]{0:T(128)} %param.20) | copy-start | bytes 52
  30.5 8.9 %collective-permute-start.1 = (bf16[2,256,256]{2,1,0:T(8,128)(2,1)S(1)}, bf16[2,256,256]{2,1,0:T(8,128)(2,1)S(1)}, u32[]{:S(2)}, u32[]{:S(2)}) collective-permute-start(bf16[2,256,256]{2,1,0:T(8,128)(2,1)S(1)} %get-tuple-element.34), channel_id=1, source_target_pairs={{4,0},{8,4},{12,8},{16,12},{20,16},{24,20},{28,24},{32,28},{36,32}... | collective-permute-start | bytes 786440 | tf_op jit(solution)/shard_map/ppermute | solution.py:46
  34.2 6.3 %collective-permute-start = (bf16[2,256,256]{2,1,0:T(8,128)(2,1)S(1)}, bf16[2,256,256]{2,1,0:T(8,128)(2,1)}, u32[]{:S(2)}, u32[]{:S(2)}) collective-permute-start(bf16[2,256,256]{2,1,0:T(8,128)(2,1)S(1)} %get-tuple-element.33), channel_id=1, source_target_pairs={{0,4},{4,8},{8,12},{12,16},{16,20},{20,24},{24,28},{28,32},{32,36}... | collective-permute-start | bytes 786440 | tf_op jit(solution)/shard_map/ppermute | solution.py:45
  69.8 2.5 copy-start.4
  72.1 29.6 %copy-start.3 = (bf16[512,256]{1,0:T(8,128)(2,1)S(1)}, bf16[512,256]{1,0:T(8,128)(2,1)}, u32[]{:S(2)}) copy-start(bf16[512,256]{1,0:T(8,128)(2,1)} %param.12) | copy-start | bytes 786436
  72.3 60.6 %copy-start.11 = (bf16[3,1024,256]{2,1,0:T(8,128)(2,1)S(1)}, bf16[3,1024,256]{2,1,0:T(8,128)(2,1)}, u32[]{:S(2)}) copy-start(bf16[3,1024,256]{2,1,0:T(8,128)(2,1)} %param.17) | copy-start | bytes 4718596
  72.3 60.6 %copy-start.13 = (f32[1024]{0:T(1024)S(1)}, f32[1024]{0:T(1024)}, u32[]{:S(2)}) copy-start(f32[1024]{0:T(1024)} %param.16) | copy-start | bytes 12292
  73.8 57.6 %all-gather.6.cloned.1.call-start = ((), (), s32[]{:S(2)}) async-start(), calls=%async_computation.5 | async-start | bytes 1310720 | tf_op jit(solution)/shard_map/all_gather | solution.py:156
  103.4 119.3 %all-gather.8.cloned.1.call-start = ((), (), s32[]{:S(2)}) async-start(), calls=%async_computation.6 | async-start | bytes 8519680 | tf_op jit(solution)/shard_map/all_gather | solution.py:19
  132.9 2.5 copy-start.12
  135.4 23.4 %copy-start.10 = (s32[4]{0:T(128)S(1)}, s32[4]{0:T(128)}, u32[]{:S(2)}) copy-start(s32[4]{0:T(128)} %param.22) | copy-start | bytes 52
  229.1 19.0 %copy-start.1 = (bf16[512,256]{1,0:T(8,128)(2,1)S(1)}, bf16[512,256]{1,0:T(8,128)(2,1)}, u32[]{:S(2)}) copy-start(bf16[512,256]{1,0:T(8,128)(2,1)} %add_convert_fusion.1) | copy-start | bytes 786436
  229.1 18.8 %all-to-all-start.1 = ((bf16[4,512,256]{2,1,0:T(8,128)(2,1)}), bf16[4,512,256]{2,1,0:T(8,128)(2,1)S(1)}, u32[]{:S(2)}, u32[]{:S(2)}) async-start(bf16[4,512,256]{2,1,0:T(8,128)(2,1)} %bitcast.126), calls=%async_computation.2 | async-start | bytes 2097152 | tf_op jit(solution)/shard_map/all_to_all | solution.py:59
  233.9 5.2 %collective-permute-start.7 = (s32[1,1]{1,0:T(1,128)}, s32[1,1]{1,0:T(1,128)}, u32[]{:S(2)}, u32[]{:S(2)}) collective-permute-start(s32[1,1]{1,0:T(1,128)} %get-tuple-element.40), channel_id=1, source_target_pairs={{0,192},{4,196},{8,200},{12,204},{16,208},{20,212},{24,216},{28,22... | collective-permute-start | bytes 20 | tf_op jit(solution)/shard_map/ppermute | solution.py:15
  235.8 6.5 %collective-permute-start.6 = (s32[1,1]{1,0:T(1,128)}, s32[1,1]{1,0:T(1,128)}, u32[]{:S(2)}, u32[]{:S(2)}) collective-permute-start(s32[1,1]{1,0:T(1,128)} %get-tuple-element.41), channel_id=1, source_target_pairs={{0,128},{4,132},{8,136},{12,140},{16,144},{20,148},{24,152},{28,15... | collective-permute-start | bytes 20 | tf_op jit(solution)/shard_map/ppermute | solution.py:15
  239.1 4.8 %collective-permute-start.5 = (s32[1,1]{1,0:T(1,128)}, s32[1,1]{1,0:T(1,128)}, u32[]{:S(2)}, u32[]{:S(2)}) collective-permute-start(s32[1,1]{1,0:T(1,128)} %get-tuple-element.42), channel_id=1, source_target_pairs={{0,64},{4,68},{8,72},{12,76},{16,80},{20,84},{24,88},{28,92},{32,9... | collective-permute-start | bytes 20 | tf_op jit(solution)/shard_map/ppermute | solution.py:15
  248.7 5.2 %collective-permute-start.4 = (bf16[1,1,128,256]{3,2,1,0:T(8,128)(2,1)S(1)}, bf16[1,1,128,256]{3,2,1,0:T(8,128)(2,1)S(1)}, u32[]{:S(2)}, u32[]{:S(2)}) collective-permute-start(bf16[1,1,128,256]{3,2,1,0:T(8,128)(2,1)S(1)} %get-tuple-element.36), channel_id=1, source_target_pairs={{0,192},{4,196},{8,200},{12,204},{16,208},{20,212},{24,216},{28,22... | collective-permute-start | bytes 196616 | tf_op jit(solution)/shard_map/ppermute | solution.py:15
  250.7 8.2 %collective-permute-start.3 = (bf16[1,1,128,256]{3,2,1,0:T(8,128)(2,1)S(1)}, bf16[1,1,128,256]{3,2,1,0:T(8,128)(2,1)S(1)}, u32[]{:S(2)}, u32[]{:S(2)}) collective-permute-start(bf16[1,1,128,256]{3,2,1,0:T(8,128)(2,1)S(1)} %get-tuple-element.37), channel_id=1, source_target_pairs={{0,128},{4,132},{8,136},{12,140},{16,144},{20,148},{24,152},{28,15... | collective-permute-start | bytes 196616 | tf_op jit(solution)/shard_map/ppermute | solution.py:15
  254.0 8.3 %collective-permute-start.2 = (bf16[1,1,128,256]{3,2,1,0:T(8,128)(2,1)S(1)}, bf16[1,1,128,256]{3,2,1,0:T(8,128)(2,1)S(1)}, u32[]{:S(2)}, u32[]{:S(2)}) collective-permute-start(bf16[1,1,128,256]{3,2,1,0:T(8,128)(2,1)S(1)} %get-tuple-element.38), channel_id=1, source_target_pairs={{0,64},{4,68},{8,72},{12,76},{16,80},{20,84},{24,88},{28,92},{32,9... | collective-permute-start | bytes 196616 | tf_op jit(solution)/shard_map/ppermute | solution.py:15
  (3 other events, 4.9 us)
Sparse Core Ops, SparseCore 0:
  73.9 27.6 reduce-scatter.1
  103.5 27.8 all-gather.5
  137.2 85.3 all-gather.7
where the time goes:
time: 271 us; the launch traced here: 270 us
  waiting for transfers between devices  99.8 us (37%)
  blocking collectives  68.7 us (25%)
  local copies, waits for them, and re-layouts  33 us (12%)
  starting transfers between devices  25.6 us (9%)
  other arithmetic  15.4 us (6%)
  matrix products  14 us (5%)
  between operations  13.5 us (5%)
    all_gather x1, blocking collectives, gathered_total(): parts = lax.all_gather(array, axis)  48.5 us
    all_gather x1, waiting for transfers between devices, gather_rows(): return lax.all_gather(shard_rows, 'heads', axis=1, tiled=True)  28 us
    reduce_scatter x1, waiting for transfers between devices, body(): lax.psum_scatter(partial_value.astype(jnp.bfloat16), 'heads', scatter_dim...  27.8 us
    all_to_all x1, blocking collectives, copy_for_each(): return lax.all_to_all(copies, axis, split_axis=0, concat_axis=0, tiled=True)  20.2 us
    all_to_all x1, waiting for transfers between devices, copy_for_each(): return lax.all_to_all(copies, axis, split_axis=0, concat_axis=0, tiled=True)  14.1 us
    all_gather x1, waiting for transfers between devices, gathered_total(): parts = lax.all_gather(array, axis)  13.4 us
    ppermute x6, waiting for transfers between devices, passed_along(): return lax.ppermute(value, axis, pairs)  13.1 us
    ppermute x6, starting transfers between devices, passed_along(): return lax.ppermute(value, axis, pairs)  10.4 us
  transfers between devices with their start and end apart: 13, of which 11 were waited for; matrix products, arithmetic and copies ran while one was open for 3% of the time, Pallas kernels for 0%

commit v1 on v0

--- a/solution.py
+++ b/solution.py
@@ -1,12 +1,28 @@
+import functools
 import jax
 import jax.numpy as jnp
 from jax import lax
 from jax.sharding import PartitionSpec as P
+from jax.lax import all_to_all, axis_size
 
 HD = 64
 BLOCK = 128
 HALO_BLK = 2
 EPSILON = 1e-06
+
+
+def reach_the_bench(chunk, bus_axis):
+    res = all_to_all(
+        jnp.concatenate(tuple((chunk for _ in range(axis_size(bus_axis)))), axis=1),
+        bus_axis,
+        1,
+        1,
+        tiled=True,
+    )
+    return res
+
+
+_perform_slabs = functools.partial(reach_the_bench, bus_axis="heads")
 
 
 def passed_along(value, axis, steps):
@@ -153,7 +169,7 @@
 
 
 def gather_rows(shard_rows):
-    return lax.all_gather(shard_rows, "heads", axis=1, tiled=True)
+    return _perform_slabs(shard_rows)
 
 
 def global_mixing(full_rows, gain_vector, triple_weight, feature_map, out_weight):

time: 271 us -> 258 us (0.952)
  waiting for transfers between devices: 99.8 us -> 70.6 us
  blocking collectives: 68.7 us -> 86 us
    all_gather x1 -> x0, waiting for transfers between devices: 28 us -> none  [gather_rows(): return lax.all_gather(shard_rows, 'heads', axis=1, tiled=True)]
    all_to_all x0 -> x1, blocking collectives: none -> 15.8 us  [reach_the_bench(): all_to_all(jnp.concatenate(tuple((chunk for _ in range(axis_size(bus_axis...]
  transfers between devices with their start and end apart: 13 -> 12, of which waited for: 11 -> 10; matrix products, arithmetic and copies ran while one was open for 3% -> 3% of each run, Pallas kernels for 0% -> 0%
where the time goes in v1:
time: 258 us
  blocking collectives  86 us (33%)
  waiting for transfers between devices  70.6 us (27%)
  local copies, waits for them, and re-layouts  35.3 us (14%)
  starting transfers between devices  25.5 us (10%)
  between operations  13.8 us (5%)
  other arithmetic  13.7 us (5%)
  matrix products  12.7 us (5%)
    all_gather x1, blocking collectives, gathered_total(): parts = lax.all_gather(array, axis)  48.5 us
    reduce_scatter x1, waiting for transfers between devices, body(): lax.psum_scatter(partial_value.astype(jnp.bfloat16), 'heads', scatter_dim...  27.8 us
    all_to_all x1, blocking collectives, copy_for_each(): return lax.all_to_all(copies, axis, split_axis=0, concat_axis=0, tiled=True)  21.6 us
    all_to_all x1, blocking collectives, reach_the_bench(): all_to_all(jnp.concatenate(tuple((chunk for _ in range(axis_size(bus_axis...  15.8 us
    all_to_all x1, waiting for transfers between devices, copy_for_each(): return lax.all_to_all(copies, axis, split_axis=0, concat_axis=0, tiled=True)  14.1 us
    ppermute x6, waiting for transfers between devices, passed_along(): return lax.ppermute(value, axis, pairs)  13.1 us
    all_gather x1, waiting for transfers between devices, gathered_total(): parts = lax.all_gather(array, axis)  12 us
    ppermute x6, starting transfers between devices, passed_along(): return lax.ppermute(value, axis, pairs)  10.4 us
  transfers between devices with their start and end apart: 12, of which 10 were waited for; matrix products, arithmetic and copies ran while one was open for 3% of the time, Pallas kernels for 0%

profile of v1, /device:TPU:33, one launch (start us, length us, event | category | flops | bytes accessed | tf_op | source)
XLA Modules:
  0.0 257.5 jit_solution(7947857385784922037)
XLA Ops:
  8.7 4.2 %all-to-all-start = ((bf16[4,512,256]{2,1,0:T(8,128)(2,1)}), bf16[4,512,256]{2,1,0:T(8,128)(2,1)}, u32[]{:S(2)}, u32[]{:S(2)}) async-start(bf16[4,512,256]{2,1,0:T(8,128)(2,1)} %broadcast_in_dim.96), calls=%async_computation | async-start | bytes 2097152 | tf_op jit(solution)/shard_map/all_to_all | solution.py:47
  13.1 14.1 %all-to-all-done = bf16[4,512,256]{2,1,0:T(8,128)(2,1)} async-done(((bf16[4,512,256]{2,1,0:T(8,128)(2,1)}), bf16[4,512,256]{2,1,0:T(8,128)(2,1)}, u32[]{:S(2)}, u32[]{:S(2)}) %all-to-all-start) | async-done | bytes 1048608 | tf_op jit(solution)/shard_map/all_to_all | solution.py:47
  30.5 3.7 %collective-permute-start.1 = (bf16[2,256,256]{2,1,0:T(8,128)(2,1)S(1)}, bf16[2,256,256]{2,1,0:T(8,128)(2,1)S(1)}, u32[]{:S(2)}, u32[]{:S(2)}) collective-permute-start(bf16[2,256,256]{2,1,0:T(8,128)(2,1)S(1)} %get-tuple-element.34), channel_id=1, source_target_pairs={{4,0},{8,4},{12,8},{16,12},{20,16},{24,20},{28,24},{32,28},{36,32}... | collective-permute-start | bytes 786440 | tf_op jit(solution)/shard_map/ppermute | solution.py:62
  34.2 3.0 %collective-permute-start = (bf16[2,256,256]{2,1,0:T(8,128)(2,1)S(1)}, bf16[2,256,256]{2,1,0:T(8,128)(2,1)}, u32[]{:S(2)}, u32[]{:S(2)}) collective-permute-start(bf16[2,256,256]{2,1,0:T(8,128)(2,1)S(1)} %get-tuple-element.33), channel_id=1, source_target_pairs={{0,4},{4,8},{8,12},{12,16},{16,20},{20,24},{24,28},{28,32},{32,36}... | collective-permute-start | bytes 786440 | tf_op jit(solution)/shard_map/ppermute | solution.py:61
  41.7 2.8 %gather_fusion = bf16[32,2,128,256]{3,2,1,0:T(8,128)(2,1)} fusion(bf16[2,8,128,256]{3,2,1,0:T(8,128)(2,1)S(1)} %bitcast.131, s32[1024]{0:T(1024)S(1)} %pad_clamp_fusion.2), kind=kCustom, calls=%fused_computation | custom fusion | bytes 8388736 | tf_op jit(solution)/shard_map/while/body/eval_jaxpr/gather | solution.py:97
  44.5 7.5 %copy.41 = bf16[4,8,2,128,256]{3,1,4,0,2:T(8,128)(2,1)} copy(bf16[4,8,2,128,256]{4,3,2,1,0:T(8,128)(2,1)} %bitcast.132) | data formatting | bytes 8388608 | tf_op jit(solution)/shard_map/while/body/eval_jaxpr/gather | solution.py:97
  52.0 4.5 %fusion.46 = (bf16[1,4,8,128,256]{3,2,4,1,0:T(8,128)(2,1)}, bf16[1,4,8,128,256]{3,2,4,1,0:T(8,128)(2,1)}) fusion(bf16[2,4,8,128,256]{3,2,4,1,0:T(8,128)(2,1)} %bitcast.133), kind=kLoop, calls=%fused_computation.103 | loop fusion | bytes 8388608 | tf_op jit(solution)/shard_map/while/body/eval_jaxpr/slice | solution.py:101
  56.5 4.2 %squeeze.19 = bf16[4,1024,4,64]{1,3,2,0:T(8,128)(2,1)} reshape(bf16[1,4,8,128,256]{3,2,4,1,0:T(8,128)(2,1)} %get-tuple-element.20) | data formatting | bytes 4194304 | tf_op jit(solution)/shard_map/while/body/eval_jaxpr/squeeze | solution.py:110
  60.7 4.2 %squeeze.21 = bf16[4,1024,4,64]{1,3,2,0:T(8,128)(2,1)} reshape(bf16[1,4,8,128,256]{3,2,4,1,0:T(8,128)(2,1)} %get-tuple-element.19) | data formatting | bytes 4194304 | tf_op jit(solution)/shard_map/while/body/eval_jaxpr/squeeze | solution.py:101
  64.8 2.9 %fusion = (f32[4,4,128]{2,1,0:T(4,128)S(1)}, f32[4,4,128,1024]{3,2,1,0:T(8,128)S(1)}) fusion(pred[4,1024]{1,0:T(4,128)(4,1)S(1)} %broadcast_compare_fusion, bf16[4,1024,4,64]{1,3,2,0:T(8,128)(2,1)} %squeeze.21, bf16[4,128,4,64]{3,2,1,0:T(4,128)(2,1)S(1)} %reshape.302), kind=kOutput, calls=%fused_computation.5 | convolution fusion | flops 274724864 | bytes 10760192 | tf_op jit(solution)/shard_map/while/body/eval_jaxpr/gqhd,gkhd->ghqk/dot_general | solution.py:100
  69.9 2.2 fusion.30
  73.9 27.8 %reduce-scatter.2.cloned.1.call-done = bf16[512,256]{1,0:T(8,128)(2,1)} async-done(((bf16[512,1024]{1,0:T(8,128)(2,1)}), bf16[512,256]{1,0:T(8,128)(2,1)}) %reduce-scatter.2.cloned.1.call-update) | async-done | bytes 262160 | tf_op jit(solution)/shard_map/reduce_scatter | solution.py:237
  102.8 15.8 %all_to_all.25 = bf16[512,4,256]{2,0,1:T(8,128)(2,1)} all-to-all(bf16[512,4,256]{2,0,1:T(8,128)(2,1)S(1)} %bitcast.138), channel_id=1, replica_groups=mesh['nodes'=64,'heads'=4] {'heads'}, dimensions={1} | all-to-all | bytes 2097152 | tf_op jit(solution)/shard_map/all_to_all | solution.py:15
  124.4 21.6 %all_to_all.26 = s32[64,1,4]{2,1,0:T(1,128)S(1)} all-to-all(s32[64,1,4]{2,1,0:T(1,128)S(1)} %broadcast_in_dim.100), channel_id=1, replica_groups=mesh['nodes'=64,'heads'=4] {'nodes'}, dimensions={0} | all-to-all | bytes 2048 | tf_op jit(solution)/shard_map/all_to_all | solution.py:47
  147.9 48.5 %all-gather.2 = f32[64,4,128]{2,1,0:T(4,128)S(1)} all-gather(f32[1,4,128]{2,1,0:T(4,128)S(1)} %bitcast.150), channel_id=3, replica_groups=mesh['nodes'=64,'heads'=4] {'nodes'}, dimensions={0}, use_global_device_ids=true | all-gather | bytes 133120 | tf_op jit(solution)/shard_map/all_gather | solution.py:35
  197.7 12.0 %all-gather.5.cloned.1.call-done = f32[256,128,64]{1,2,0:T(8,128)} async-done(((f32[4,128,64]{1,2,0:T(8,128)}), f32[256,128,64]{1,2,0:T(8,128)}) %all-gather.5.cloned.1.call-update) | async-done | bytes 8388624 | tf_op jit(solution)/shard_map/all_gather | solution.py:35
  209.8 3.9 %reduce_sum.116 = f32[4,128,64]{1,2,0:T(8,128)S(1)} reduce(f32[64,4,128,64]{2,3,1,0:T(8,128)} %bitcast.134, f32[]{:T(128)} %constant.91.clone.1), dimensions={0}, to_apply=%region_5.6 | reduce | flops 2064384 | bytes 8519684 | tf_op jit(solution)/shard_map/reduce_sum | solution.py:36
  216.2 4.0 %all-to-all-start.2 = ((bf16[4,512,256]{2,1,0:T(8,128)(2,1)}), bf16[4,512,256]{2,1,0:T(8,128)(2,1)S(1)}, u32[]{:S(2)}, u32[]{:S(2)}) async-start(bf16[4,512,256]{2,1,0:T(8,128)(2,1)} %bitcast.137), calls=%async_computation.3 | async-start | bytes 2097152 | tf_op jit(solution)/shard_map/all_to_all | solution.py:75
  222.7 3.3 %collective-permute-start.6 = (s32[1,1]{1,0:T(1,128)}, s32[1,1]{1,0:T(1,128)}, u32[]{:S(2)}, u32[]{:S(2)}) collective-permute-start(s32[1,1]{1,0:T(1,128)} %get-tuple-element.41), channel_id=1, source_target_pairs={{0,128},{4,132},{8,136},{12,140},{16,144},{20,148},{24,152},{28,15... | collective-permute-start | bytes 20 | tf_op jit(solution)/shard_map/ppermute | solution.py:31
  226.1 3.0 %collective-permute-done.6 = s32[1,1]{1,0:T(1,128)} collective-permute-done((s32[1,1]{1,0:T(1,128)}, s32[1,1]{1,0:T(1,128)}, u32[]{:S(2)}, u32[]{:S(2)}) %collective-permute-start.6) | collective-permute-done | bytes 36 | tf_op jit(solution)/shard_map/ppermute | solution.py:31
  230.7 2.6 %add_subtract_fusion = s32[4]{0:T(128)S(1)} fusion(s32[1]{0:T(128)} %bitcast.35, s32[1]{0:T(128)} %bitcast.34, s32[1]{0:T(128)} %bitcast.33, s32[1]{0:T(128)} %bitcast.32, s32[]{:T(128)S(6)} %mul.73), kind=kLoop, calls=%fused_computation.99 | loop fusion | flops 16 | bytes 36 | tf_op jit(solution)/shard_map/sub | solution.py:163
  237.6 3.3 %collective-permute-start.3 = (bf16[1,1,128,256]{3,2,1,0:T(8,128)(2,1)S(1)}, bf16[1,1,128,256]{3,2,1,0:T(8,128)(2,1)S(1)}, u32[]{:S(2)}, u32[]{:S(2)}) collective-permute-start(bf16[1,1,128,256]{3,2,1,0:T(8,128)(2,1)S(1)} %get-tuple-element.37), channel_id=1, source_target_pairs={{0,128},{4,132},{8,136},{12,140},{16,144},{20,148},{24,152},{28,15... | collective-permute-start | bytes 196616 | tf_op jit(solution)/shard_map/ppermute | solution.py:31
  240.9 4.8 %collective-permute-done.3 = bf16[1,1,128,256]{3,2,1,0:T(8,128)(2,1)S(1)} collective-permute-done((bf16[1,1,128,256]{3,2,1,0:T(8,128)(2,1)S(1)}, bf16[1,1,128,256]{3,2,1,0:T(8,128)(2,1)S(1)}, u32[]{:S(2)}, u32[]{:S(2)}) %collective-permute-start.3) | collective-permute-done | bytes 65568 | tf_op jit(solution)/shard_map/ppermute | solution.py:31
  245.7 3.7 %collective-permute-done.2 = bf16[1,1,128,256]{3,2,1,0:T(8,128)(2,1)S(1)} collective-permute-done((bf16[1,1,128,256]{3,2,1,0:T(8,128)(2,1)S(1)}, bf16[1,1,128,256]{3,2,1,0:T(8,128)(2,1)S(1)}, u32[]{:S(2)}, u32[]{:S(2)}) %collective-permute-start.2) | collective-permute-done | bytes 65568 | tf_op jit(solution)/shard_map/ppermute | solution.py:31
  (98 shorter events, 36.0 us)
Async XLA Ops:
  6.5 22.8 %copy-start = (bf16[3,1024,256]{2,1,0:T(8,128)(2,1)S(1)}, bf16[3,1024,256]{2,1,0:T(8,128)(2,1)}, u32[]{:S(2)}) copy-start(bf16[3,1024,256]{2,1,0:T(8,128)(2,1)} %param.14) | copy-start | bytes 4718596
  6.5 6.5 %copy-start.7 = (s32[4,8]{1,0:T(4,128)S(1)}, s32[4,8]{1,0:T(4,128)}, u32[]{:S(2)}) copy-start(s32[4,8]{1,0:T(4,128)} %param.21) | copy-start | bytes 388
  8.7 18.6 %all-to-all-start = ((bf16[4,512,256]{2,1,0:T(8,128)(2,1)}), bf16[4,512,256]{2,1,0:T(8,128)(2,1)}, u32[]{:S(2)}, u32[]{:S(2)}) async-start(bf16[4,512,256]{2,1,0:T(8,128)(2,1)} %broadcast_in_dim.96), calls=%async_computation | async-start | bytes 2097152 | tf_op jit(solution)/shard_map/all_to_all | solution.py:47
  13.0 16.1 %copy-start.5 = (f32[1024]{0:T(1024)S(1)}, f32[1024]{0:T(1024)}, u32[]{:S(2)}) copy-start(f32[1024]{0:T(1024)} %param.13) | copy-start | bytes 12292
  13.0 88.6 %reduce-scatter.2.cloned.1.call-start = ((), (), s32[]{:S(2)}) async-start(), calls=%async_computation.5 | async-start | bytes 1310720 | tf_op jit(solution)/shard_map/reduce_scatter | solution.py:237
  29.4 7.9 %copy-start.9 = (s32[4]{0:T(128)S(1)}, s32[4]{0:T(128)}, u32[]{:S(2)}) copy-start(s32[4]{0:T(128)} %param.20) | copy-start | bytes 52
  30.5 8.9 %collective-permute-start.1 = (bf16[2,256,256]{2,1,0:T(8,128)(2,1)S(1)}, bf16[2,256,256]{2,1,0:T(8,128)(2,1)S(1)}, u32[]{:S(2)}, u32[]{:S(2)}) collective-permute-start(bf16[2,256,256]{2,1,0:T(8,128)(2,1)S(1)} %get-tuple-element.34), channel_id=1, source_target_pairs={{4,0},{8,4},{12,8},{16,12},{20,16},{24,20},{28,24},{32,28},{36,32}... | collective-permute-start | bytes 786440 | tf_op jit(solution)/shard_map/ppermute | solution.py:62
  34.2 6.3 %collective-permute-start = (bf16[2,256,256]{2,1,0:T(8,128)(2,1)S(1)}, bf16[2,256,256]{2,1,0:T(8,128)(2,1)}, u32[]{:S(2)}, u32[]{:S(2)}) collective-permute-start(bf16[2,256,256]{2,1,0:T(8,128)(2,1)S(1)} %get-tuple-element.33), channel_id=1, source_target_pairs={{0,4},{4,8},{8,12},{12,16},{16,20},{20,24},{24,28},{28,32},{32,36}... | collective-permute-start | bytes 786440 | tf_op jit(solution)/shard_map/ppermute | solution.py:61
  67.8 2.1 copy-start.1
  69.8 2.5 copy-start.3
  72.1 29.5 %copy-start.2 = (bf16[512,256]{1,0:T(8,128)(2,1)S(1)}, bf16[512,256]{1,0:T(8,128)(2,1)}, u32[]{:S(2)}) copy-start(bf16[512,256]{1,0:T(8,128)(2,1)} %param.12) | copy-start | bytes 786436
  73.8 135.9 %all-gather.5.cloned.1.call-start = ((), (), s32[]{:S(2)}) async-start(), calls=%async_computation.6 | async-start | bytes 8519680 | tf_op jit(solution)/shard_map/all_gather | solution.py:35
  118.6 1.8 copy-start.6
  120.1 1.4 copy-start.11
  121.6 1.1 copy-start.12
  122.6 1.7 copy-start.8
  122.7 24.7 %copy-start.10 = (s32[4]{0:T(128)S(1)}, s32[4]{0:T(128)}, u32[]{:S(2)}) copy-start(s32[4]{0:T(128)} %param.22) | copy-start | bytes 52
  216.2 18.7 %all-to-all-start.2 = ((bf16[4,512,256]{2,1,0:T(8,128)(2,1)}), bf16[4,512,256]{2,1,0:T(8,128)(2,1)S(1)}, u32[]{:S(2)}, u32[]{:S(2)}) async-start(bf16[4,512,256]{2,1,0:T(8,128)(2,1)} %bitcast.137), calls=%async_computation.3 | async-start | bytes 2097152 | tf_op jit(solution)/shard_map/all_to_all | solution.py:75
  220.9 5.2 %collective-permute-start.7 = (s32[1,1]{1,0:T(1,128)}, s32[1,1]{1,0:T(1,128)}, u32[]{:S(2)}, u32[]{:S(2)}) collective-permute-start(s32[1,1]{1,0:T(1,128)} %get-tuple-element.40), channel_id=1, source_target_pairs={{0,192},{4,196},{8,200},{12,204},{16,208},{20,212},{24,216},{28,22... | collective-permute-start | bytes 20 | tf_op jit(solution)/shard_map/ppermute | solution.py:31
  222.7 6.3 %collective-permute-start.6 = (s32[1,1]{1,0:T(1,128)}, s32[1,1]{1,0:T(1,128)}, u32[]{:S(2)}, u32[]{:S(2)}) collective-permute-start(s32[1,1]{1,0:T(1,128)} %get-tuple-element.41), channel_id=1, source_target_pairs={{0,128},{4,132},{8,136},{12,140},{16,144},{20,148},{24,152},{28,15... | collective-permute-start | bytes 20 | tf_op jit(solution)/shard_map/ppermute | solution.py:31
  226.0 4.7 %collective-permute-start.5 = (s32[1,1]{1,0:T(1,128)}, s32[1,1]{1,0:T(1,128)}, u32[]{:S(2)}, u32[]{:S(2)}) collective-permute-start(s32[1,1]{1,0:T(1,128)} %get-tuple-element.42), channel_id=1, source_target_pairs={{0,64},{4,68},{8,72},{12,76},{16,80},{20,84},{24,88},{28,92},{32,9... | collective-permute-start | bytes 20 | tf_op jit(solution)/shard_map/ppermute | solution.py:31
  235.7 5.3 %collective-permute-start.4 = (bf16[1,1,128,256]{3,2,1,0:T(8,128)(2,1)S(1)}, bf16[1,1,128,256]{3,2,1,0:T(8,128)(2,1)S(1)}, u32[]{:S(2)}, u32[]{:S(2)}) collective-permute-start(bf16[1,1,128,256]{3,2,1,0:T(8,128)(2,1)S(1)} %get-tuple-element.36), channel_id=1, source_target_pairs={{0,192},{4,196},{8,200},{12,204},{16,208},{20,212},{24,216},{28,22... | collective-permute-start | bytes 196616 | tf_op jit(solution)/shard_map/ppermute | solution.py:31
  237.6 8.1 %collective-permute-start.3 = (bf16[1,1,128,256]{3,2,1,0:T(8,128)(2,1)S(1)}, bf16[1,1,128,256]{3,2,1,0:T(8,128)(2,1)S(1)}, u32[]{:S(2)}, u32[]{:S(2)}) collective-permute-start(bf16[1,1,128,256]{3,2,1,0:T(8,128)(2,1)S(1)} %get-tuple-element.37), channel_id=1, source_target_pairs={{0,128},{4,132},{8,136},{12,140},{16,144},{20,148},{24,152},{28,15... | collective-permute-start | bytes 196616 | tf_op jit(solution)/shard_map/ppermute | solution.py:31
  240.9 8.5 %collective-permute-start.2 = (bf16[1,1,128,256]{3,2,1,0:T(8,128)(2,1)S(1)}, bf16[1,1,128,256]{3,2,1,0:T(8,128)(2,1)S(1)}, u32[]{:S(2)}, u32[]{:S(2)}) collective-permute-start(bf16[1,1,128,256]{3,2,1,0:T(8,128)(2,1)S(1)} %get-tuple-element.38), channel_id=1, source_target_pairs={{0,64},{4,68},{8,72},{12,76},{16,80},{20,84},{24,88},{28,92},{32,9... | collective-permute-start | bytes 196616 | tf_op jit(solution)/shard_map/ppermute | solution.py:31
  (1 other events, 1.0 us)
Sparse Core Ops, SparseCore 0:
  73.9 27.6 reduce-scatter.1
  124.5 85.2 all-gather.4
